TPU v7x, 32 devices: a whole 2x2x4 slice. The times are simulated.
32 devices in a mesh: dp: 8 (over y, x, core), head: 4 (over z).
Axes of the slice: x: 2, y: 2, z: 4, core: 2. Of those that a mesh axis runs over, the one named last changes fastest.
Arguments:
- layer_input_rows: bfloat16 [16384, 1024], P(('dp', 'head')), may hold values from -6 to 6
- cotangent: bfloat16 [16384, 1024], P(('dp', 'head')), may hold values from -6 to 6
- lengths: int32 [16], P('dp'), may hold values from 128 to 1024, as said below
- layernorm_gain: float32 [2, 1024], P(None, ('dp', 'head')), may hold values from 0.5 to 1.5
- layernorm_bias: float32 [2, 1024], P(None, ('dp', 'head')), may hold values from -1.5 to 1.5
- frozen_projection_weight: float32 [1024, 3, 1024], P('dp', None, 'head'), may hold values from -0.1875 to 0.1875
- projection_bias: float32 [3, 16, 64], P(None, 'head', 'dp'), may hold values from -1.5 to 1.5
- adapter_project_first: float32 [3, 1024, 128], P(None, ('dp', 'head')), may hold values from -0.1875 to 0.1875
- adapter_project_second: float32 [3, 128, 1024], P(None, 'dp', 'head'), may hold values from -0.5 to 0.5
- frozen_output_weight: float32 [1024, 1024], P('head', 'dp'), may hold values from -0.75 to 0.75
- adapter_output_first: float32 [1024, 128], P('head', 'dp'), may hold values from -0.75 to 0.75
- adapter_output_second: float32 [128, 1024], P(None, ('dp', 'head')), may hold values from -0.5 to 0.5
- frozen_up_weight: float32 [1024, 4096], P('dp', 'head'), may hold values from -0.1875 to 0.1875
- hidden_bias: float32 [64, 64], P('head', 'dp'), may hold values from -1.5 to 1.5
- adapter_up_first: float32 [1024, 128], P(('dp', 'head')), may hold values from -0.1875 to 0.1875
- adapter_up_second: float32 [128, 4096], P('dp', 'head'), may hold values from -0.5 to 0.5
- frozen_down_weight: float32 [4096, 1024], P('head', 'dp'), may hold values from -0.09375 to 0.09375
- adapter_down_first: float32 [4096, 128], P('head', 'dp'), may hold values from -0.09375 to 0.09375
- adapter_down_second: float32 [128, 1024], P(None, ('dp', 'head')), may hold values from -0.5 to 0.5
- branch_output_bias: float32 [2, 1024], P(None, ('dp', 'head')), may hold values from -1.5 to 1.5
Outputs:
- layer_output: bfloat16 [16384, 1024], P(('dp', 'head'))
- grad_input: float32 [16384, 1024], P(('dp', 'head'))
- gradient_layernorm_gain: float32 [2, 1024], P(None, ('dp', 'head'))
- gradient_layernorm_bias: float32 [2, 1024], P(None, ('dp', 'head'))
- gradient_projection_bias: float32 [3, 16, 64], P(None, 'head', 'dp')
- gradient_adapter_project_first: float32 [3, 1024, 128], P(None, ('dp', 'head'))
- gradient_adapter_project_second: float32 [3, 128, 1024], P(None, 'dp', 'head')
- gradient_adapter_output_first: float32 [1024, 128], P('head', 'dp')
- gradient_adapter_output_second: float32 [128, 1024], P(None, ('dp', 'head'))
- gradient_hidden_bias: float32 [64, 64], P('head', 'dp')
- gradient_adapter_up_first: float32 [1024, 128], P(('dp', 'head'))
- gradient_adapter_up_second: float32 [128, 4096], P('dp', 'head')
- gradient_adapter_down_first: float32 [4096, 128], P('head', 'dp')
- gradient_adapter_down_second: float32 [128, 1024], P(None, ('dp', 'head'))
- gradient_branch_bias: float32 [2, 1024], P(None, ('dp', 'head'))
Inputs may be any that keep to these rules, and one draw needn't show every extreme that they name: lengths[i] counts the real tokens at the start of sequence i; the slots after them are padding; some sequence has exactly 1024.
All inputs are finite; a program needn't handle non-finite values.
Results may differ from a plain program's by a relative error of at most 0.012.
Values may be sent and summed in bfloat16 or wider, within the bound.
A program may use at most 192 MiB of HBM per device.

v0:
```python
from functools import partial
import math

import jax
import jax.numpy as jnp
from jax import lax
from jax.sharding import PartitionSpec as P

HD = 64
ADAPTER_RANK = 128
ADAPTER_ALPHA = 32
ROW_LEN = 1024
SEQS = 2


NORM_EPSILON = 1e-05
NEG_FILL = -1e30


def matrix_product(left, right):
    return jnp.dot(left, right, preferred_element_type=jnp.float32)


def rotary_tables():
    turned = HD // 4
    half_turn = turned // 2
    freqs = 10000.0 ** (-(jnp.arange(half_turn, dtype=jnp.float32) * 2.0 / turned))
    angles = jnp.arange(ROW_LEN, dtype=jnp.float32)[:, None] * freqs[None, :]
    return (jnp.cos(angles)[:, None, :], jnp.sin(angles)[:, None, :])


def turn(values, cosine, sine):
    half_turn = cosine.shape[-1]
    first = values[..., :half_turn]
    second = values[..., half_turn : 2 * half_turn]
    rest = values[..., 2 * half_turn :]
    return jnp.concatenate(
        [first * cosine - second * sine, second * cosine + first * sine, rest], axis=-1
    )


def layernorm_forward(rows):
    values = rows.astype(jnp.float32)
    centered_rows = values - jnp.mean(values, axis=-1, keepdims=True)
    inverse_scale = lax.rsqrt(
        jnp.mean(centered_rows * centered_rows, axis=-1, keepdims=True) + NORM_EPSILON
    )
    return (centered_rows * inverse_scale, inverse_scale)


def layernorm_backward(
    gradient_attention_rows,
    gradient_feedforward_rows,
    standardized_rows,
    inverse_scale,
    gain_values,
):
    gradient_standardized = (
        gradient_attention_rows * gain_values[0] + gradient_feedforward_rows * gain_values[1]
    )
    inner_product = gradient_standardized - jnp.mean(gradient_standardized, axis=-1, keepdims=True)
    inner_product = inner_product - standardized_rows * jnp.mean(
        gradient_standardized * standardized_rows, axis=-1, keepdims=True
    )
    gain_gradient_list = jnp.stack(
        [
            jnp.sum(gradient_attention_rows * standardized_rows, 0),
            jnp.sum(gradient_feedforward_rows * standardized_rows, 0),
        ]
    )
    shift_grads = jnp.stack(
        [jnp.sum(gradient_attention_rows, 0), jnp.sum(gradient_feedforward_rows, 0)]
    )
    return (inverse_scale * inner_product, gain_gradient_list, shift_grads)


def block_scores(queries, keys, offset):
    score_scale = 1.0 / math.sqrt(queries.shape[-1])
    raw = (
        jnp.einsum("qhd,khd->hqk", queries, keys, preferred_element_type=jnp.float32) * score_scale
    )
    query_pos = offset + jnp.arange(queries.shape[0])
    allowed = jnp.arange(keys.shape[0])[None, :] <= query_pos[:, None]
    return (jnp.where(allowed[None], raw, NEG_FILL), allowed, query_pos, score_scale)


def attend_block(queries, keys, values, offset, length):
    scores, allowed, query_pos, score_scale = block_scores(queries, keys, offset)
    peak = jnp.max(scores, axis=-1, keepdims=True)
    powers = jnp.exp(scores - peak)
    running_totals = jnp.sum(powers, axis=-1, keepdims=True)
    weights = (powers / running_totals).astype(jnp.bfloat16)
    attention_context = jnp.einsum(
        "hqk,khd->qhd", weights, values, preferred_element_type=jnp.float32
    )
    valid = (query_pos < length).astype(jnp.float32)
    return (
        (attention_context * valid[:, None, None]).astype(jnp.bfloat16),
        (peak + jnp.log(running_totals))[..., 0],
    )


def attend_block_back(queries, keys, values, gradient_context_rows, log_totals, offset, length):
    scores, allowed, query_pos, score_scale = block_scores(queries, keys, offset)
    weights = jnp.where(allowed[None], jnp.exp(scores - log_totals[..., None]), 0.0)
    valid = (query_pos < length).astype(jnp.bfloat16)
    grad_masked = gradient_context_rows * valid[:, None, None]
    grad_weights = jnp.einsum(
        "qhd,khd->hqk", grad_masked, values, preferred_element_type=jnp.float32
    )
    grad_values = jnp.einsum(
        "hqk,qhd->khd",
        weights.astype(jnp.bfloat16),
        grad_masked,
        preferred_element_type=jnp.float32,
    )
    mean_term = jnp.sum(weights * grad_weights, axis=-1, keepdims=True)
    grad_scores = (weights * (grad_weights - mean_term)).astype(jnp.bfloat16)
    grad_queries = (
        jnp.einsum("hqk,khd->qhd", grad_scores, keys, preferred_element_type=jnp.float32)
        * score_scale
    )
    grad_keys = (
        jnp.einsum("hqk,qhd->khd", grad_scores, queries, preferred_element_type=jnp.float32)
        * score_scale
    )
    return (grad_queries, grad_keys, grad_values)


def attend_row(row):
    queries, keys, values, length = row
    block = queries.shape[0] // 2
    first, first_total = attend_block(queries[:block], keys[:block], values[:block], 0, length)

    def later():
        return attend_block(queries[block:], keys, values, block, length)

    second, second_total = later()
    return (jnp.concatenate([first, second], axis=0), jnp.stack([first_total, second_total]))


def attend_row_back(row):
    queries, keys, values, gradient_context_rows, log_totals, length = row
    block = queries.shape[0] // 2
    first_q, first_k, first_v = attend_block_back(
        queries[:block],
        keys[:block],
        values[:block],
        gradient_context_rows[:block],
        log_totals[0],
        0,
        length,
    )

    def later():
        return attend_block_back(
            queries[block:],
            keys,
            values,
            gradient_context_rows[block:],
            log_totals[1],
            block,
            length,
        )

    second_q, second_k, second_v = later()
    padding = ((0, block), (0, 0), (0, 0))
    grad_queries = jnp.concatenate([first_q, second_q], axis=0)
    grad_keys = second_k + jnp.pad(first_k, padding)
    grad_values = second_v + jnp.pad(first_v, padding)
    return (grad_queries, grad_keys, grad_values)


def shards(
    layer_input_rows,
    cotangent,
    lengths,
    layernorm_gain,
    layernorm_bias,
    frozen_projection_weight,
    projection_bias,
    adapter_project_first,
    adapter_project_second,
    frozen_output_weight,
    adapter_output_first,
    adapter_output_second,
    frozen_up_weight,
    hidden_bias,
    adapter_up_first,
    adapter_up_second,
    frozen_down_weight,
    adapter_down_first,
    adapter_down_second,
    branch_output_bias,
):
    reduced_dtype = jnp.bfloat16
    adapter_scale = ADAPTER_ALPHA / ADAPTER_RANK
    (
        projection_weight_frozen,
        projection_bias_heads,
        projection_adapter_second,
        output_weight_frozen,
        outproj_adapter_first,
        up_weight_frozen,
        hidden_bias_row,
        up_adapter_second,
        down_weight_frozen,
        down_adapter_first,
    ) = (
        lax.all_gather(frozen_projection_weight.astype(reduced_dtype), "dp", axis=0, tiled=True),
        lax.all_gather(projection_bias.astype(reduced_dtype), "dp", axis=2, tiled=True),
        lax.all_gather(adapter_project_second.astype(reduced_dtype), "dp", axis=1, tiled=True),
        lax.all_gather(frozen_output_weight.astype(reduced_dtype), "dp", axis=1, tiled=True),
        lax.all_gather(adapter_output_first.astype(reduced_dtype), "dp", axis=1, tiled=True),
        lax.all_gather(frozen_up_weight.astype(reduced_dtype), "dp", axis=0, tiled=True),
        lax.all_gather(hidden_bias.astype(reduced_dtype), "dp", axis=1, tiled=True),
        lax.all_gather(adapter_up_second.astype(reduced_dtype), "dp", axis=0, tiled=True),
        lax.all_gather(frozen_down_weight.astype(reduced_dtype), "dp", axis=1, tiled=True),
        lax.all_gather(adapter_down_first.astype(reduced_dtype), "dp", axis=1, tiled=True),
    )
    (
        gain_values,
        shift_values,
        output_shift_value,
        projection_adapter_first,
        outproj_adapter_second,
        up_adapter_first,
        down_adapter_second,
    ) = (
        lax.all_gather(layernorm_gain.astype(reduced_dtype), ("dp", "head"), axis=1, tiled=True),
        lax.all_gather(layernorm_bias.astype(reduced_dtype), ("dp", "head"), axis=1, tiled=True),
        lax.all_gather(
            branch_output_bias.astype(reduced_dtype), ("dp", "head"), axis=1, tiled=True
        ),
        lax.all_gather(
            adapter_project_first.astype(reduced_dtype), ("dp", "head"), axis=1, tiled=True
        ),
        lax.all_gather(
            adapter_output_second.astype(reduced_dtype), ("dp", "head"), axis=1, tiled=True
        ),
        lax.all_gather(adapter_up_first.astype(reduced_dtype), ("dp", "head"), axis=0, tiled=True),
        lax.all_gather(
            adapter_down_second.astype(reduced_dtype), ("dp", "head"), axis=1, tiled=True
        ),
    )
    gain_values = gain_values.astype(jnp.float32)
    shift_values = shift_values.astype(jnp.float32)
    output_shift_value = output_shift_value.astype(jnp.float32)
    heads_local = projection_weight_frozen.shape[2] // HD
    group_rows = SEQS * ROW_LEN
    standardized_local, inverse_deviation_local = layernorm_forward(layer_input_rows)
    attention_normed, feedforward_normed = (
        lax.all_gather(
            (standardized_local * gain_values[0] + shift_values[0]).astype(reduced_dtype),
            "head",
            axis=0,
            tiled=True,
        ),
        lax.all_gather(
            (standardized_local * gain_values[1] + shift_values[1]).astype(reduced_dtype),
            "head",
            axis=0,
            tiled=True,
        ),
    )
    projection_lowrank = jnp.einsum(
        "po,von->pvn",
        attention_normed,
        projection_adapter_first,
        preferred_element_type=jnp.float32,
    ).astype(reduced_dtype)
    projected_rows = jnp.einsum(
        "td,dce->tce",
        attention_normed,
        projection_weight_frozen,
        preferred_element_type=jnp.float32,
    )
    projected_rows = projected_rows + projection_bias_heads.astype(jnp.float32).reshape(
        3, heads_local * HD
    )
    projected_rows = projected_rows + adapter_scale * jnp.einsum(
        "qpf,pfo->qpo",
        projection_lowrank,
        projection_adapter_second,
        preferred_element_type=jnp.float32,
    )
    projected_rows = projected_rows.reshape(SEQS, ROW_LEN, 3, heads_local, HD)
    cosine, sine = rotary_tables()
    queries = turn(projected_rows[:, :, 0], cosine, sine).astype(reduced_dtype)
    keys = turn(projected_rows[:, :, 1], cosine, sine).astype(reduced_dtype)
    values = projected_rows[:, :, 2].astype(reduced_dtype)
    attention_context, log_totals = lax.map(attend_row, (queries, keys, values, lengths))
    attention_context = attention_context.reshape(group_rows, heads_local * HD)
    attention_lowrank = matrix_product(attention_context, outproj_adapter_first).astype(
        reduced_dtype
    )
    up_lowrank = matrix_product(feedforward_normed, up_adapter_first).astype(reduced_dtype)
    preactivation = (
        matrix_product(feedforward_normed, up_weight_frozen)
        + hidden_bias_row.astype(jnp.float32).reshape(-1)
        + adapter_scale * matrix_product(up_lowrank, up_adapter_second)
    )
    hidden_units_rows = jax.nn.gelu(preactivation, approximate=False).astype(reduced_dtype)
    down_lowrank = matrix_product(hidden_units_rows, down_adapter_first).astype(reduced_dtype)
    running_total = matrix_product(attention_context, output_weight_frozen) + matrix_product(
        hidden_units_rows, down_weight_frozen
    )
    branch_sum = lax.psum_scatter(
        (
            running_total
            + adapter_scale
            * (
                matrix_product(attention_lowrank, outproj_adapter_second)
                + matrix_product(down_lowrank, down_adapter_second)
            )
        ).astype(jnp.bfloat16),
        "head",
        scatter_dimension=0,
        tiled=True,
    ).astype(jnp.float32)
    layer_output = (
        layer_input_rows.astype(jnp.float32)
        + branch_sum
        + output_shift_value[0]
        + output_shift_value[1]
    ).astype(reduced_dtype)
    gradient_complete = lax.all_gather(cotangent, "head", axis=0, tiled=True)
    gradient_attention_lowrank = (
        adapter_scale * matrix_product(gradient_complete, outproj_adapter_second.T)
    ).astype(reduced_dtype)
    gradient_down_lowrank = (
        adapter_scale * matrix_product(gradient_complete, down_adapter_second.T)
    ).astype(reduced_dtype)
    gradient_outproj_first = matrix_product(attention_context.T, gradient_attention_lowrank)
    gradient_outproj_second = adapter_scale * matrix_product(attention_lowrank.T, gradient_complete)
    gradient_down_first = matrix_product(hidden_units_rows.T, gradient_down_lowrank)
    gradient_down_second = adapter_scale * matrix_product(down_lowrank.T, gradient_complete)
    gradient_context_rows = (
        matrix_product(gradient_complete, output_weight_frozen.T)
        + matrix_product(gradient_attention_lowrank, outproj_adapter_first.T)
    ).astype(reduced_dtype)
    gradient_hidden_rows = matrix_product(gradient_complete, down_weight_frozen.T) + matrix_product(
        gradient_down_lowrank, down_adapter_first.T
    )
    gelu_value, gelu_pull = jax.vjp(partial(jax.nn.gelu, approximate=False), preactivation)
    gradient_preactivation = gelu_pull(gradient_hidden_rows)[0].astype(reduced_dtype)
    g_up_bias = jnp.sum(gradient_preactivation, axis=0, dtype=jnp.float32).reshape(
        hidden_bias_row.shape
    )
    gradient_up_second = adapter_scale * matrix_product(up_lowrank.T, gradient_preactivation)
    gradient_up_lowrank = (
        adapter_scale * matrix_product(gradient_preactivation, up_adapter_second.T)
    ).astype(reduced_dtype)
    gradient_up_first = matrix_product(feedforward_normed.T, gradient_up_lowrank)
    gradient_feedforward_normed = matrix_product(
        gradient_preactivation, up_weight_frozen.T
    ) + matrix_product(gradient_up_lowrank, up_adapter_first.T)
    grad_rows_ctx = gradient_context_rows.reshape(SEQS, ROW_LEN, heads_local, HD)
    grad_queries, grad_keys, grad_values = lax.map(
        attend_row_back, (queries, keys, values, grad_rows_ctx, log_totals, lengths)
    )
    grad_queries = turn(grad_queries, cosine, -sine)
    grad_keys = turn(grad_keys, cosine, -sine)
    gradient_projected_rows = jnp.stack([grad_queries, grad_keys, grad_values], axis=2)
    gradient_projected_rows = gradient_projected_rows.reshape(
        group_rows, 3, heads_local * HD
    ).astype(reduced_dtype)
    g_qkv_bias = jnp.sum(gradient_projected_rows, axis=0, dtype=jnp.float32).reshape(
        projection_bias_heads.shape
    )
    gradient_projection_second = adapter_scale * jnp.einsum(
        "tcr,tce->cre",
        projection_lowrank,
        gradient_projected_rows,
        preferred_element_type=jnp.float32,
    )
    gradient_projection_lowrank = (
        adapter_scale
        * jnp.einsum(
            "zwo,wbo->zwb",
            gradient_projected_rows,
            projection_adapter_second,
            preferred_element_type=jnp.float32,
        )
    ).astype(reduced_dtype)
    gradient_projection_first = jnp.einsum(
        "td,tcr->cdr",
        attention_normed,
        gradient_projection_lowrank,
        preferred_element_type=jnp.float32,
    )
    grad_normed_a = jnp.einsum(
        "tce,dce->td",
        gradient_projected_rows,
        projection_weight_frozen,
        preferred_element_type=jnp.float32,
    )
    grad_normed_a = grad_normed_a + jnp.einsum(
        "oxa,xja->oj",
        gradient_projection_lowrank,
        projection_adapter_first,
        preferred_element_type=jnp.float32,
    )
    gradient_attention_local, gradient_feedforward_local = (
        lax.psum_scatter(
            grad_normed_a.astype(jnp.bfloat16), "head", scatter_dimension=0, tiled=True
        ).astype(jnp.float32),
        lax.psum_scatter(
            gradient_feedforward_normed.astype(jnp.bfloat16),
            "head",
            scatter_dimension=0,
            tiled=True,
        ).astype(jnp.float32),
    )
    gradient_row_list, gradient_gain_values, gradient_shift_values = layernorm_backward(
        gradient_attention_local,
        gradient_feedforward_local,
        standardized_local,
        inverse_deviation_local,
        gain_values,
    )
    cot_float = cotangent.astype(jnp.float32)
    grad_input = cot_float + gradient_row_list
    bias_row = jnp.sum(cot_float, axis=0)
    g_out_bias = jnp.stack([bias_row, bias_row])
    (
        gradient_projection_bias,
        gradient_adapter_project_second,
        gradient_adapter_output_first,
        gradient_hidden_bias,
        gradient_adapter_up_second,
        gradient_adapter_down_first,
    ) = (
        lax.psum_scatter(g_qkv_bias, "dp", scatter_dimension=2, tiled=True),
        lax.psum_scatter(gradient_projection_second, "dp", scatter_dimension=1, tiled=True),
        lax.psum_scatter(gradient_outproj_first, "dp", scatter_dimension=1, tiled=True),
        lax.psum_scatter(g_up_bias, "dp", scatter_dimension=1, tiled=True),
        lax.psum_scatter(gradient_up_second, "dp", scatter_dimension=0, tiled=True),
        lax.psum_scatter(gradient_down_first, "dp", scatter_dimension=1, tiled=True),
    )
    (
        gradient_layernorm_gain,
        gradient_layernorm_bias,
        gradient_branch_bias,
        gradient_adapter_project_first,
        gradient_adapter_output_second,
        gradient_adapter_up_first,
        gradient_adapter_down_second,
    ) = (
        lax.psum_scatter(gradient_gain_values, ("dp", "head"), scatter_dimension=1, tiled=True),
        lax.psum_scatter(gradient_shift_values, ("dp", "head"), scatter_dimension=1, tiled=True),
        lax.psum_scatter(g_out_bias, ("dp", "head"), scatter_dimension=1, tiled=True),
        lax.psum_scatter(
            gradient_projection_first, ("dp", "head"), scatter_dimension=1, tiled=True
        ),
        lax.psum_scatter(gradient_outproj_second, ("dp", "head"), scatter_dimension=1, tiled=True),
        lax.psum_scatter(gradient_up_first, ("dp", "head"), scatter_dimension=0, tiled=True),
        lax.psum_scatter(gradient_down_second, ("dp", "head"), scatter_dimension=1, tiled=True),
    )
    return (
        layer_output,
        grad_input,
        gradient_layernorm_gain,
        gradient_layernorm_bias,
        gradient_projection_bias,
        gradient_adapter_project_first,
        gradient_adapter_project_second,
        gradient_adapter_output_first,
        gradient_adapter_output_second,
        gradient_hidden_bias,
        gradient_adapter_up_first,
        gradient_adapter_up_second,
        gradient_adapter_down_first,
        gradient_adapter_down_second,
        gradient_branch_bias,
    )


def solution(mesh):
    in_specs = (
        P(("dp", "head"), None),
        P(("dp", "head"), None),
        P("dp"),
        P(None, ("dp", "head")),
        P(None, ("dp", "head")),
        P("dp", None, "head"),
        P(None, "head", "dp"),
        P(None, ("dp", "head"), None),
        P(None, "dp", "head"),
        P("head", "dp"),
        P("head", "dp"),
        P(None, ("dp", "head")),
        P("dp", "head"),
        P("head", "dp"),
        P(("dp", "head"), None),
        P("dp", "head"),
        P("head", "dp"),
        P("head", "dp"),
        P(None, ("dp", "head")),
        P(None, ("dp", "head")),
    )
    out_specs = (
        P(("dp", "head"), None),
        P(("dp", "head"), None),
        P(None, ("dp", "head")),
        P(None, ("dp", "head")),
        P(None, "head", "dp"),
        P(None, ("dp", "head"), None),
        P(None, "dp", "head"),
        P("head", "dp"),
        P(None, ("dp", "head")),
        P("head", "dp"),
        P(("dp", "head"), None),
        P("dp", "head"),
        P("head", "dp"),
        P(None, ("dp", "head")),
        P(None, ("dp", "head")),
    )
    return jax.shard_map(shards, mesh=mesh, in_specs=in_specs, out_specs=out_specs, check_vma=False)
```

profile of v0, /device:TPU:0, one launch (start us, length us, event | category | flops | bytes accessed | tf_op | source)
XLA Modules:
  0.0 2022.9 jit_solution(4759980592173767980)
XLA Ops:
  11.8 69.8 %all-gather.1 = bf16[32,32,2]{1,2,0:T(2,128)(2,1)S(1)} all-gather(bf16[1,32,2]{1,2,0:T(2,128)(2,1)S(1)} %convert_bitcast_fusion.1), channel_id=1, replica_groups=mesh['dp'=8,'head'=4] {'dp','head'}, dimensions={0}, use_global_device_ids=true | all-gather | bytes 4224 | tf_op jit(solution)/shard_map/all_gather | solution.py:231
  81.6 63.4 %all-gather = bf16[32,32,2]{1,2,0:T(2,128)(2,1)S(1)} all-gather(bf16[1,32,2]{1,2,0:T(2,128)(2,1)S(1)} %convert_bitcast_fusion.2), channel_id=1, replica_groups=mesh['dp'=8,'head'=4] {'dp','head'}, dimensions={0}, use_global_device_ids=true | all-gather | bytes 4224 | tf_op jit(solution)/shard_map/all_gather | solution.py:230
  209.3 75.9 %all_gather.77 = bf16[128,1024]{0,1:T(8,128)(2,1)} all-gather(bf16[128,32]{0,1:T(8,128)(2,1)S(1)} %convert_element_type.252), channel_id=1, replica_groups=mesh['dp'=8,'head'=4] {'dp','head'}, dimensions={1}, use_global_device_ids=true | all-gather | bytes 270336 | tf_op jit(solution)/shard_map/all_gather | solution.py:242
  285.2 75.6 %all_gather.71 = bf16[1024,128]{1,0:T(8,128)(2,1)} all-gather(bf16[32,128]{1,0:T(8,128)(2,1)S(1)} %convert_element_type.242), channel_id=1, replica_groups=mesh['dp'=8,'head'=4] {'dp','head'}, dimensions={0}, use_global_device_ids=true | all-gather | bytes 270336 | tf_op jit(solution)/shard_map/all_gather | solution.py:241
  360.8 75.1 %all_gather.75 = bf16[128,1024]{0,1:T(8,128)(2,1)S(1)} all-gather(bf16[128,32]{0,1:T(8,128)(2,1)S(1)} %convert_element_type.249), channel_id=1, replica_groups=mesh['dp'=8,'head'=4] {'dp','head'}, dimensions={1}, use_global_device_ids=true | all-gather | bytes 270336 | tf_op jit(solution)/shard_map/all_gather | solution.py:238
  445.5 70.8 %all_gather.65 = bf16[3,1024,128]{2,1,0:T(8,128)(2,1)S(1)} all-gather(bf16[3,32,128]{2,1,0:T(8,128)(2,1)S(1)} %convert_element_type.234), channel_id=1, replica_groups=mesh['dp'=8,'head'=4] {'dp','head'}, dimensions={1}, use_global_device_ids=true | all-gather | bytes 811008 | tf_op jit(solution)/shard_map/all_gather | solution.py:235
  573.8 25.3 %while.28 = (s32[]{:T(128)}, bf16[2,1024,4,64]{1,3,2,0:T(8,128)(2,1)}, f32[2,2,4,512]{3,2,1,0:T(4,128)S(1)}, bf16[2,1024,4,64]{1,3,2,0:T(8,128)(2,1)}, bf16[2,10...) while((s32[]{:T(128)}, ...), condition=%wide.region_7.8_spmd, body=%wide.region_2.7_spmd.sunk | while | flops 845417472 | bytes 57326316 | solution.py:292
  599.1 43.7 %while.29 = (s32[]{:T(128)}, f32[2,1024,4,64]{1,3,2,0:T(8,128)}, f32[2,1024,4,64]{1,3,2,0:T(8,128)}, bf16[2,1024,4,64]{1,3,2,0:T(8,128)(2,1)}, bf16[2,1024,4,64]...) while((s32[]{:T(128)}, f32[2,1024,4,64]{1,3,2,0:T(8,128)}, ...), condition=%wide.region_12.13_spmd, body=%wide.region_9.12_spmd.sunk | while | flops 2048261120 | bytes 153979296 | solution.py:359
  686.5 10.9 fusion.138
  704.8 21.9 %multiply_convert_fusion.2 = (bf16[2048,1024]{1,0:T(8,128)(2,1)}, f32[2048,1024]{1,0:T(8,128)}, f32[2048,1024]{1,0:T(8,128)}) fusion(bf16[2048,128]{1,0:T(8,128)(2,1)S(1)} %convolution_convert_fusion.2, bf16[128,1024]{1,0:T(8,128)(2,1)S(1)} %copy-done.44, f32[2048,1024]{1,0:T(8,128)S(1)} %copy-done.75, f32[1024]{0:T(1024)S(1)} %copy-done.65), kind=kOutput, calls=%fused_computation.122 | convolution fusion | flops 679477248 | bytes 30150656 | tf_op jit(solution)/shard_map/dot_general | solution.py:21
  773.0 67.3 %all-gather.2 = bf16[32,32,2]{1,2,0:T(2,128)(2,1)S(1)} all-gather(bf16[1,32,2]{1,2,0:T(2,128)(2,1)S(1)} %convert_bitcast_fusion), channel_id=1, replica_groups=mesh['dp'=8,'head'=4] {'dp','head'}, dimensions={0}, use_global_device_ids=true | all-gather | bytes 4224 | tf_op jit(solution)/shard_map/all_gather | solution.py:232
  855.7 57.4 %reduce-scatter.24.cloned.1.call-done = bf16[512,1024]{1,0:T(8,128)(2,1)} async-done(((bf16[2048,1024]{1,0:T(8,128)(2,1)}), bf16[512,1024]{1,0:T(8,128)(2,1)}) %reduce-scatter.24.cloned.1.call-update) | async-done | bytes 1048592 | tf_op jit(solution)/shard_map/reduce_scatter | solution.py:308
  949.7 24.2 %all-reduce.5 = (f32[3,4,64]{2,1,0:T(4,128)S(1)}, f32[16,64]{1,0:T(8,128)S(1)}) all-reduce(f32[3,4,64]{2,1,0:T(4,128)S(1)} %reshape.321, f32[16,64]{1,0:T(8,128)S(1)} %reshape.322), channel_id=7, replica_groups=mesh['dp'=8,'head'=4] {'dp'}, use_global_device_ids=true, to_apply=%region_24.25.clone | all-reduce | flops 1792 | bytes 14336
  975.3 78.2 %all-reduce.8.cloned.1.call-done = f32[3,1024,128]{2,0,1:T(4,128)} async-done(((f32[3,1024,128]{2,0,1:T(4,128)}), f32[3,1024,128]{2,0,1:T(4,128)}) %all-reduce.8.cloned.1.call-update) | async-done | bytes 1572880
  1055.0 135.8 %reduce-scatter.44.cloned.1.call-done = f32[32,2]{1,0:T(8,128)} async-done(((f32[1024,2]{1,0:T(8,128)}), f32[32,2]{1,0:T(8,128)}) %reduce-scatter.44.cloned.1.call-update) | async-done | bytes 272
  1192.1 133.3 %reduce-scatter.42.cloned.1.call-done = f32[32,2]{1,0:T(8,128)} async-done(((f32[1024,2]{1,0:T(8,128)}), f32[32,2]{1,0:T(8,128)}) %reduce-scatter.42.cloned.1.call-update) | async-done | bytes 272
  1326.7 133.4 %reduce-scatter.48.cloned.1.call-done = f32[32,2]{1,0:T(8,128)} async-done(((f32[1024,2]{1,0:T(8,128)}), f32[32,2]{1,0:T(8,128)}) %reduce-scatter.48.cloned.1.call-update) | async-done | bytes 272
  1461.5 32.0 %reduce-scatter.32.cloned.1.call-done = f32[256,16]{0,1:T(8,128)} async-done(((f32[256,128]{0,1:T(8,128)}), f32[256,16]{0,1:T(8,128)}) %reduce-scatter.32.cloned.1.call-update) | async-done | bytes 16400 | tf_op jit(solution)/shard_map/reduce_scatter | solution.py:436
  1493.4 37.4 %reduce-scatter.30.cloned.1.call-done = f32[3,16,256]{2,1,0:T(8,128)} async-done(((f32[3,128,256]{2,1,0:T(8,128)}), f32[3,16,256]{2,1,0:T(8,128)}) %reduce-scatter.30.cloned.1.call-update) | async-done | bytes 49168 | tf_op jit(solution)/shard_map/reduce_scatter | solution.py:435
  1530.8 37.7 %reduce-scatter.38.cloned.1.call-done = f32[1024,16]{0,1:T(8,128)} async-done(((f32[1024,128]{0,1:T(8,128)}), f32[1024,16]{0,1:T(8,128)}) %reduce-scatter.38.cloned.1.call-update) | async-done | bytes 65552 | tf_op jit(solution)/shard_map/reduce_scatter | solution.py:439
  1568.5 37.7 %reduce-scatter.46.cloned.1.call-done = f32[16,1024]{1,0:T(8,128)} async-done(((f32[128,1024]{1,0:T(8,128)}), f32[16,1024]{1,0:T(8,128)}) %reduce-scatter.46.cloned.1.call-update) | async-done | bytes 65552
  1606.1 138.9 %reduce-scatter.34.cloned.1.call-done = f32[128,32]{0,1:T(8,128)} async-done(((f32[128,1024]{0,1:T(8,128)}), f32[128,32]{0,1:T(8,128)}) %reduce-scatter.34.cloned.1.call-update) | async-done | bytes 16400 | tf_op jit(solution)/shard_map/reduce_scatter | solution.py:456
  1745.0 135.3 %reduce-scatter.36.cloned.1.call-done = f32[32,128]{1,0:T(8,128)} async-done(((f32[1024,128]{1,0:T(8,128)}), f32[32,128]{1,0:T(8,128)}) %reduce-scatter.36.cloned.1.call-update) | async-done | bytes 16400 | tf_op jit(solution)/shard_map/reduce_scatter | solution.py:457
  1880.4 135.2 %reduce-scatter.40.cloned.1.call-done = f32[128,32]{0,1:T(8,128)} async-done(((f32[128,1024]{0,1:T(8,128)}), f32[128,32]{0,1:T(8,128)}) %reduce-scatter.40.cloned.1.call-update) | async-done | bytes 16400 | tf_op jit(solution)/shard_map/reduce_scatter | solution.py:458
  (425 shorter events, 358.2 us)
Async XLA Ops:
  7.2 142.0 %copy-start.40 = (f32[128,3,256]{2,0,1:T(8,128)S(1)}, f32[128,3,256]{2,0,1:T(8,128)}, u32[]{:S(2)}) copy-start(f32[128,3,256]{2,0,1:T(8,128)} %param.29) | copy-start | bytes 1179652
  7.2 509.1 %all-gather.10.cloned.1.call-start = ((), (), s32[]{:S(2)}) async-start(), calls=%async_computation.13 | async-start | bytes 5242880 | tf_op jit(solution)/shard_map/all_gather | solution.py:253
  149.1 372.0 %all-gather.12.cloned.1.call-start = ((), (), s32[]{:S(2)}) async-start(), calls=%async_computation.14 | async-start | bytes 1769472 | tf_op jit(solution)/shard_map/all_gather | solution.py:210
  149.9 405.8 %all-gather.20.cloned.1.call-start = ((), (), s32[]{:S(2)}) async-start(), calls=%async_computation.19 | async-start | bytes 5242880 | tf_op jit(solution)/shard_map/all_gather | solution.py:327
  150.7 531.8 %all-gather.14.cloned.1.call-start = ((), (), s32[]{:S(2)}) async-start(), calls=%async_computation.15 | async-start | bytes 5242880 | tf_op jit(solution)/shard_map/all_gather | solution.py:259
  151.2 535.3 %all-gather.16.cloned.1.call-start = ((), (), s32[]{:S(2)}) async-start(), calls=%async_computation.16 | async-start | bytes 2359296 | tf_op jit(solution)/shard_map/all_gather | solution.py:215
  152.1 545.3 %all-gather.18.cloned.1.call-start = ((), (), s32[]{:S(2)}) async-start(), calls=%async_computation.17 | async-start | bytes 2359296 | tf_op jit(solution)/shard_map/all_gather | solution.py:218
  152.9 697.0 %reduce-scatter.26.cloned.1.call-start = ((), (), s32[]{:S(2)}) async-start(), calls=%async_computation.20 | async-start | bytes 5242880 | tf_op jit(solution)/shard_map/reduce_scatter | solution.py:405
  171.2 389.4 %copy-start.34 = (bf16[256,128]{0,1:T(8,128)(2,1)}, bf16[256,128]{0,1:T(8,128)(2,1)S(1)}, u32[]{:S(2)}) copy-start(bf16[256,128]{0,1:T(8,128)(2,1)S(1)} %all_gather.74) | copy-start | bytes 196612
  180.5 387.9 %copy-start.41 = (f32[1024,8]{0,1:T(8,128)}, f32[1024,8]{0,1:T(8,128)S(1)}, u32[]{:S(2)}) copy-start(f32[1024,8]{0,1:T(8,128)S(1)} %get-tuple-element.457) | copy-start | bytes 98308
  189.8 337.5 %copy-start.32 = (bf16[3,128,256]{2,1,0:T(8,128)(2,1)}, bf16[3,128,256]{2,1,0:T(8,128)(2,1)S(1)}, u32[]{:S(2)}) copy-start(bf16[3,128,256]{2,1,0:T(8,128)(2,1)S(1)} %all_gather.66) | copy-start | bytes 589828
  678.1 171.9 %reduce-scatter.28.cloned.1.call-start = ((), (), s32[]{:S(2)}) async-start(), calls=%async_computation.21 | async-start | bytes 5242880 | tf_op jit(solution)/shard_map/reduce_scatter | solution.py:408
  746.3 166.8 %reduce-scatter.24.cloned.1.call-start = ((), (), s32[]{:S(2)}) async-start(), calls=%async_computation.18 | async-start | bytes 5242880 | tf_op jit(solution)/shard_map/reduce_scatter | solution.py:308
  772.4 281.1 %all-reduce.8.cloned.1.call-start = ((), (), s32[]{:S(2)}) async-start(), calls=%async_computation.32 | async-start | bytes 4194304
  849.9 340.9 %reduce-scatter.44.cloned.1.call-start = ((), (), s32[]{:S(2)}) async-start(), calls=%async_computation.29 | async-start | bytes 540672
  854.2 471.2 %reduce-scatter.42.cloned.1.call-start = ((), (), s32[]{:S(2)}) async-start(), calls=%async_computation.28 | async-start | bytes 540672
  855.3 604.8 %reduce-scatter.48.cloned.1.call-start = ((), (), s32[]{:S(2)}) async-start(), calls=%async_computation.31 | async-start | bytes 540672
  918.2 575.2 %reduce-scatter.32.cloned.1.call-start = ((), (), s32[]{:S(2)}) async-start(), calls=%async_computation.23 | async-start | bytes 147456 | tf_op jit(solution)/shard_map/reduce_scatter | solution.py:436
  920.5 610.3 %reduce-scatter.30.cloned.1.call-start = ((), (), s32[]{:S(2)}) async-start(), calls=%async_computation.22 | async-start | bytes 442368 | tf_op jit(solution)/shard_map/reduce_scatter | solution.py:435
  924.5 644.0 %reduce-scatter.38.cloned.1.call-start = ((), (), s32[]{:S(2)}) async-start(), calls=%async_computation.26 | async-start | bytes 589824 | tf_op jit(solution)/shard_map/reduce_scatter | solution.py:439
  928.4 677.7 %reduce-scatter.46.cloned.1.call-start = ((), (), s32[]{:S(2)}) async-start(), calls=%async_computation.30 | async-start | bytes 589824
  933.5 811.5 %reduce-scatter.34.cloned.1.call-start = ((), (), s32[]{:S(2)}) async-start(), calls=%async_computation.24 | async-start | bytes 540672 | tf_op jit(solution)/shard_map/reduce_scatter | solution.py:456
  938.3 942.0 %reduce-scatter.36.cloned.1.call-start = ((), (), s32[]{:S(2)}) async-start(), calls=%async_computation.25 | async-start | bytes 540672 | tf_op jit(solution)/shard_map/reduce_scatter | solution.py:457
  942.7 1072.9 %reduce-scatter.40.cloned.1.call-start = ((), (), s32[]{:S(2)}) async-start(), calls=%async_computation.27 | async-start | bytes 540672 | tf_op jit(solution)/shard_map/reduce_scatter | solution.py:458
  (82 other events, 1069.0 us)
Sparse Core Ops, SparseCore 0:
  149.3 80.0 all-gather.9
  231.3 24.2 all-gather.11
  257.1 85.4 all-gather.19
  344.6 84.0 all-gather.13
  430.5 27.0 all-gather.15
  459.3 28.2 all-gather.17
  678.2 75.4 reduce-scatter.25
  756.0 77.5 reduce-scatter.27
  835.9 77.0 reduce-scatter.23
  918.2 135.1 all-reduce.7
  1055.7 134.9 reduce-scatter.43
  1192.9 132.4 reduce-scatter.41
  1327.6 132.4 reduce-scatter.47
  1463.5 29.8 reduce-scatter.31
  1496.9 33.8 reduce-scatter.29
  1534.3 34.1 reduce-scatter.37
  1572.0 34.1 reduce-scatter.45
  1608.8 136.1 reduce-scatter.33
  1747.8 132.4 reduce-scatter.35
  1883.0 132.4 reduce-scatter.39
where the time goes:
time: 2030 us; the launch traced here: 2020 us
  waiting for transfers between devices  1090 us (54%)
  blocking collectives  586 us (29%)
  matrix products  192 us (9%)
  local copies, waits for them, and re-layouts  89.9 us (4%)
  other arithmetic  41.7 us (2%)
    unnamed x25, waiting for transfers between devices  520 us
    reduce_scatter x1, waiting for transfers between devices, shards(): lax.psum_scatter(gradient_outproj_second, ('dp', 'head'), scatter_dimensi...  139 us
    reduce_scatter x1, waiting for transfers between devices, shards(): lax.psum_scatter(gradient_up_first, ('dp', 'head'), scatter_dimension=0,...  135 us
    reduce_scatter x1, waiting for transfers between devices, shards(): lax.psum_scatter(gradient_down_second, ('dp', 'head'), scatter_dimension=...  135 us
    dot_general x24, matrix products, matrix_product(): return jnp.dot(left, right, preferred_element_type=jnp.float32)  118 us
    all_gather x1, blocking collectives, shards(): lax.all_gather(adapter_down_second.astype(reduced_dtype), ('dp', 'head'),...  75.9 us
    all_gather x1, blocking collectives, shards(): lax.all_gather(adapter_up_first.astype(reduced_dtype), ('dp', 'head'), ax...  75.6 us
    all_gather x1, blocking collectives, shards(): lax.all_gather(adapter_output_second.astype(reduced_dtype), ('dp', 'head'...  75.1 us
  transfers between devices with their start and end apart: 20, of which 12 were waited for; matrix products, arithmetic and copies ran while one was open for 15% of the time, Pallas kernels for 0%

commit v1 on v0

v1 whole, which is shorter than its diff:
```python
from functools import partial
import math

import jax
import jax.numpy as jnp
from jax import lax
from jax.sharding import PartitionSpec as P

HD = 64
ADAPTER_RANK = 128
ADAPTER_ALPHA = 32
ROW_LEN = 1024
SEQS = 2


NORM_EPSILON = 1e-05
NEG_FILL = -1e30


def matrix_product(left, right):
    return jnp.dot(left, right, preferred_element_type=jnp.float32)


def rotary_tables():
    turned = HD // 4
    half_turn = turned // 2
    freqs = 10000.0 ** (-(jnp.arange(half_turn, dtype=jnp.float32) * 2.0 / turned))
    angles = jnp.arange(ROW_LEN, dtype=jnp.float32)[:, None] * freqs[None, :]
    return (jnp.cos(angles)[:, None, :], jnp.sin(angles)[:, None, :])


def turn(values, cosine, sine):
    half_turn = cosine.shape[-1]
    first = values[..., :half_turn]
    second = values[..., half_turn : 2 * half_turn]
    rest = values[..., 2 * half_turn :]
    return jnp.concatenate(
        [first * cosine - second * sine, second * cosine + first * sine, rest], axis=-1
    )


def layernorm_forward(rows):
    values = rows.astype(jnp.float32)
    centered_rows = values - jnp.mean(values, axis=-1, keepdims=True)
    inverse_scale = lax.rsqrt(
        jnp.mean(centered_rows * centered_rows, axis=-1, keepdims=True) + NORM_EPSILON
    )
    return (centered_rows * inverse_scale, inverse_scale)


def block_scores(queries, keys, offset):
    score_scale = 1.0 / math.sqrt(queries.shape[-1])
    raw = (
        jnp.einsum("qhd,khd->hqk", queries, keys, preferred_element_type=jnp.float32) * score_scale
    )
    query_pos = offset + jnp.arange(queries.shape[0])
    allowed = jnp.arange(keys.shape[0])[None, :] <= query_pos[:, None]
    return (jnp.where(allowed[None], raw, NEG_FILL), allowed, query_pos, score_scale)


def attend_block(queries, keys, values, offset, length):
    scores, allowed, query_pos, score_scale = block_scores(queries, keys, offset)
    peak = jnp.max(scores, axis=-1, keepdims=True)
    powers = jnp.exp(scores - peak)
    running_totals = jnp.sum(powers, axis=-1, keepdims=True)
    weights = (powers / running_totals).astype(jnp.bfloat16)
    attention_context = jnp.einsum(
        "hqk,khd->qhd", weights, values, preferred_element_type=jnp.float32
    )
    valid = (query_pos < length).astype(jnp.float32)
    return (
        (attention_context * valid[:, None, None]).astype(jnp.bfloat16),
        (peak + jnp.log(running_totals))[..., 0],
    )


def attend_block_back(queries, keys, values, gradient_context_rows, log_totals, offset, length):
    scores, allowed, query_pos, score_scale = block_scores(queries, keys, offset)
    weights = jnp.where(allowed[None], jnp.exp(scores - log_totals[..., None]), 0.0)
    valid = (query_pos < length).astype(jnp.bfloat16)
    grad_masked = gradient_context_rows * valid[:, None, None]
    grad_weights = jnp.einsum(
        "qhd,khd->hqk", grad_masked, values, preferred_element_type=jnp.float32
    )
    grad_values = jnp.einsum(
        "hqk,qhd->khd",
        weights.astype(jnp.bfloat16),
        grad_masked,
        preferred_element_type=jnp.float32,
    )
    mean_term = jnp.sum(weights * grad_weights, axis=-1, keepdims=True)
    grad_scores = (weights * (grad_weights - mean_term)).astype(jnp.bfloat16)
    grad_queries = (
        jnp.einsum("hqk,khd->qhd", grad_scores, keys, preferred_element_type=jnp.float32)
        * score_scale
    )
    grad_keys = (
        jnp.einsum("hqk,qhd->khd", grad_scores, queries, preferred_element_type=jnp.float32)
        * score_scale
    )
    return (grad_queries, grad_keys, grad_values)


def attend_row(row):
    queries, keys, values, length = row
    block = queries.shape[0] // 2
    first, first_total = attend_block(queries[:block], keys[:block], values[:block], 0, length)

    def later():
        return attend_block(queries[block:], keys, values, block, length)

    second, second_total = later()
    return (jnp.concatenate([first, second], axis=0), jnp.stack([first_total, second_total]))


def attend_row_back(row):
    queries, keys, values, gradient_context_rows, log_totals, length = row
    block = queries.shape[0] // 2
    first_q, first_k, first_v = attend_block_back(
        queries[:block],
        keys[:block],
        values[:block],
        gradient_context_rows[:block],
        log_totals[0],
        0,
        length,
    )

    def later():
        return attend_block_back(
            queries[block:],
            keys,
            values,
            gradient_context_rows[block:],
            log_totals[1],
            block,
            length,
        )

    second_q, second_k, second_v = later()
    padding = ((0, block), (0, 0), (0, 0))
    grad_queries = jnp.concatenate([first_q, second_q], axis=0)
    grad_keys = second_k + jnp.pad(first_k, padding)
    grad_values = second_v + jnp.pad(first_v, padding)
    return (grad_queries, grad_keys, grad_values)


def shards(
    layer_input_rows,
    cotangent,
    lengths,
    layernorm_gain,
    layernorm_bias,
    frozen_projection_weight,
    projection_bias,
    adapter_project_first,
    adapter_project_second,
    frozen_output_weight,
    adapter_output_first,
    adapter_output_second,
    frozen_up_weight,
    hidden_bias,
    adapter_up_first,
    adapter_up_second,
    frozen_down_weight,
    adapter_down_first,
    adapter_down_second,
    branch_output_bias,
):
    low = jnp.bfloat16
    f32 = jnp.float32
    scale = ADAPTER_ALPHA / ADAPTER_RANK
    n_dp = lax.axis_size("dp")
    n_head = lax.axis_size("head")
    width = layer_input_rows.shape[1]
    head_width = frozen_projection_weight.shape[2]
    heads_local = head_width // HD
    hidden = frozen_up_weight.shape[1]
    depth = frozen_projection_weight.shape[0]
    factor_rows = adapter_project_second.shape[1]
    own_rows = adapter_up_first.shape[0]
    group_rows = SEQS * ROW_LEN
    rank = ADAPTER_RANK

    rows_all = lax.all_gather(layer_input_rows, "head", axis=0, tiled=True)

    main = jnp.concatenate(
        [
            jnp.concatenate(
                [
                    frozen_projection_weight.astype(low).reshape(depth, 3 * head_width),
                    frozen_up_weight.astype(low),
                    frozen_output_weight.astype(low).T,
                    frozen_down_weight.astype(low).T,
                ],
                axis=1,
            ),
            jnp.concatenate(
                [
                    adapter_project_second.astype(low).transpose(1, 0, 2).reshape(factor_rows, 3 * head_width),
                    adapter_up_second.astype(low),
                    adapter_output_first.astype(low).T,
                    adapter_down_first.astype(low).T,
                ],
                axis=1,
            ),
        ],
        axis=0,
    )
    shared = jnp.concatenate(
        [
            adapter_project_first.astype(low).reshape(3 * own_rows, rank),
            adapter_up_first.astype(low),
            adapter_output_second.astype(low).T,
            adapter_down_second.astype(low).T,
        ],
        axis=0,
    )
    small = jnp.stack([layernorm_gain, layernorm_bias, branch_output_bias]).astype(low).reshape(-1)
    biases = jnp.concatenate([projection_bias.astype(low).reshape(-1), hidden_bias.astype(low).reshape(-1)])

    def as_rows(flat):
        count = -(-flat.shape[0] // (16 * rank)) * 16 * rank
        return jnp.pad(flat, (0, count - flat.shape[0])).reshape(-1, rank)

    shared = jnp.concatenate([shared, as_rows(small)], axis=0)
    shared_rows = shared.shape[0]
    shared = lax.all_gather(shared, "head", axis=0, tiled=True)
    shared = jnp.concatenate([shared, as_rows(biases)], axis=0)
    shared = lax.all_gather(shared, "dp", axis=0, tiled=False)
    main = lax.all_gather(main, "dp", axis=0, tiled=False)

    bias_part = shared[:, n_head * shared_rows :].reshape(n_dp, -1)
    shared = shared[:, : n_head * shared_rows].reshape(n_dp * n_head, shared_rows, rank)
    span = projection_bias.shape[2]
    n_proj = 3 * heads_local * span
    proj_bias = bias_part[:, :n_proj].reshape(n_dp, 3, heads_local, span).transpose(1, 2, 0, 3).reshape(3 * head_width).astype(f32)
    n_hid = hidden_bias.shape[0] * span
    hid_bias = bias_part[:, n_proj : n_proj + n_hid].reshape(n_dp, -1, span).transpose(1, 0, 2).reshape(hidden).astype(f32)
    three = 3 * own_rows
    proj_first = shared[:, :three].reshape(n_dp * n_head, 3, own_rows, rank).transpose(1, 0, 2, 3).reshape(3, width, rank)
    up_first = shared[:, three : three + own_rows].reshape(width, rank)
    out_second_t = shared[:, three + own_rows : three + 2 * own_rows].reshape(width, rank)
    down_second_t = shared[:, three + 2 * own_rows : three + 3 * own_rows].reshape(width, rank)
    smalls = shared[:, three + 3 * own_rows :].reshape(n_dp * n_head, -1)[:, : 6 * own_rows]
    smalls = smalls.reshape(n_dp * n_head, 3, 2, own_rows).transpose(1, 2, 0, 3).reshape(3, 2, width).astype(f32)
    gain, shift, out_shift = smalls[0], smalls[1], smalls[2]

    frozen = main[:, :depth].reshape(width, -1)
    factors = main[:, depth:].reshape(rank, -1)
    c1, c2, c3 = 3 * head_width, 3 * head_width + hidden, 4 * head_width + hidden
    w_proj, w_up, w_out_t, w_down_t = frozen[:, :c1], frozen[:, c1:c2], frozen[:, c2:c3], frozen[:, c3:]
    proj_second, up_second = factors[:, :c1], factors[:, c1:c2]
    out_first_t, down_first_t = factors[:, c2:c3], factors[:, c3:]

    def mm(left, right):
        return jnp.dot(left, right, preferred_element_type=f32)

    def mm_t(left, right):
        return lax.dot_general(left, right, (((1,), (1,)), ((), ())), preferred_element_type=f32)

    def tmm(left, right):
        return lax.dot_general(left, right, (((0,), (0,)), ((), ())), preferred_element_type=f32)

    standard, inverse = layernorm_forward(rows_all)
    normed_a = (standard * gain[0] + shift[0]).astype(low)
    normed_m = (standard * gain[1] + shift[1]).astype(low)
    low_qkv = [mm(normed_a, proj_first[c]).astype(low) for c in range(3)]
    cosine, sine = rotary_tables()
    projected = []
    for c in range(3):
        cut = slice(c * head_width, (c + 1) * head_width)
        part = mm(normed_a, w_proj[:, cut]) + proj_bias[cut] + scale * mm(low_qkv[c], proj_second[:, cut])
        part = part.reshape(SEQS, ROW_LEN, heads_local, HD)
        projected.append((turn(part, cosine, sine) if c < 2 else part).astype(low))
    queries, keys, values = projected
    context, log_totals = lax.map(attend_row, (queries, keys, values, lengths))
    context = context.reshape(group_rows, head_width)
    attn_low = mm_t(context, out_first_t).astype(low)
    up_low = mm(normed_m, up_first).astype(low)
    preact = mm(normed_m, w_up) + hid_bias + scale * mm(up_low, up_second)
    units = jax.nn.gelu(preact, approximate=False).astype(low)
    down_low = mm_t(units, down_first_t).astype(low)
    branch = mm_t(context, w_out_t) + mm_t(units, w_down_t)
    branch = branch + scale * (mm_t(attn_low, out_second_t) + mm_t(down_low, down_second_t))
    branch_sum = lax.psum_scatter(branch.astype(low), "head", scatter_dimension=0, tiled=True)
    layer_output = (
        layer_input_rows.astype(f32) + branch_sum.astype(f32) + out_shift[0] + out_shift[1]
    ).astype(low)

    cot = lax.all_gather(cotangent, "head", axis=0, tiled=True)
    g_attn_low = (scale * mm(cot, out_second_t)).astype(low)
    g_down_low = (scale * mm(cot, down_second_t)).astype(low)
    d_out_first_t = tmm(g_attn_low, context)
    d_out_second_t = scale * tmm(cot, attn_low)
    d_down_first_t = tmm(g_down_low, units)
    d_down_second_t = scale * tmm(cot, down_low)
    g_context = (mm(cot, w_out_t) + mm(g_attn_low, out_first_t)).astype(low)
    g_hidden = mm(cot, w_down_t) + mm(g_down_low, down_first_t)
    _, pull = jax.vjp(partial(jax.nn.gelu, approximate=False), preact)
    g_pre = pull(g_hidden)[0].astype(low)
    d_hid_bias = jnp.sum(g_pre, axis=0, dtype=f32)
    d_up_second = scale * tmm(up_low, g_pre)
    g_up_low = (scale * mm_t(g_pre, up_second)).astype(low)
    d_up_first = tmm(normed_m, g_up_low)
    g_normed_m = mm_t(g_pre, w_up) + mm_t(g_up_low, up_first)
    g_rows = g_context.reshape(SEQS, ROW_LEN, heads_local, HD)
    g_q, g_k, g_v = lax.map(attend_row_back, (queries, keys, values, g_rows, log_totals, lengths))
    g_parts = [turn(g_q, cosine, -sine), turn(g_k, cosine, -sine), g_v]
    g_parts = [g.reshape(group_rows, head_width).astype(low) for g in g_parts]
    d_proj_bias = jnp.concatenate([jnp.sum(g, axis=0, dtype=f32) for g in g_parts])
    g_normed_a = 0.0
    d_proj_second, d_proj_first = [], []
    for c in range(3):
        cut = slice(c * head_width, (c + 1) * head_width)
        g = g_parts[c]
        d_proj_second.append(scale * tmm(low_qkv[c], g))
        g_low = (scale * mm_t(g, proj_second[:, cut])).astype(low)
        d_proj_first.append(tmm(normed_a, g_low))
        g_normed_a = g_normed_a + mm_t(g, w_proj[:, cut]) + mm_t(g_low, proj_first[c])
    g_standard = (g_normed_a * gain[0] + g_normed_m * gain[1]).astype(low)
    d_gain = jnp.stack([jnp.sum(g_normed_a * standard, 0), jnp.sum(g_normed_m * standard, 0)])
    d_shift = jnp.stack([jnp.sum(g_normed_a, 0), jnp.sum(g_normed_m, 0)])
    cot_own = cotangent.astype(f32)
    bias_row = jnp.sum(cot_own, axis=0)
    d_branch = jnp.stack([bias_row, bias_row])

    g_own = lax.psum_scatter(g_standard, "head", scatter_dimension=0, tiled=True).astype(f32)
    own_standard, own_inverse = layernorm_forward(layer_input_rows)
    inner = g_own - jnp.mean(g_own, axis=-1, keepdims=True)
    inner = inner - own_standard * jnp.mean(g_own * own_standard, axis=-1, keepdims=True)
    grad_input = cot_own + own_inverse * inner

    per_head = jnp.concatenate(d_proj_second + [d_up_second, d_out_first_t, d_down_first_t], axis=1)
    all_rows = n_dp * n_head
    small = jnp.stack([d_gain, d_shift, d_branch]).reshape(3, 2, all_rows, own_rows).transpose(2, 0, 1, 3)
    small = small.reshape(all_rows, -1)
    small = jnp.pad(small, ((0, 0), (0, 8 * rank - small.shape[1]))).reshape(all_rows, 8, rank)
    shared = jnp.concatenate(
        [
            jnp.stack(d_proj_first).reshape(3, all_rows, own_rows, rank).transpose(1, 0, 2, 3).reshape(all_rows, 3 * own_rows, rank),
            d_up_first.reshape(all_rows, own_rows, rank),
            d_out_second_t.reshape(all_rows, own_rows, rank),
            d_down_second_t.reshape(all_rows, own_rows, rank),
            small,
        ],
        axis=1,
    )
    count = shared.shape[1]
    biases = jnp.concatenate(
        [
            d_proj_bias.reshape(3 * heads_local, n_dp, span).transpose(1, 0, 2).reshape(n_dp, -1),
            d_hid_bias.reshape(-1, n_dp, span).transpose(1, 0, 2).reshape(n_dp, -1),
        ],
        axis=1,
    )
    n_bias = biases.shape[1]
    bias_rows = -(-n_bias // (8 * rank)) * 8
    biases = jnp.pad(biases, ((0, 0), (0, bias_rows * rank - n_bias))).reshape(n_dp, bias_rows, rank)
    shared = jnp.concatenate([shared.reshape(n_dp, n_head * count, rank), biases], axis=1)
    per_head = lax.psum_scatter(per_head, "dp", scatter_dimension=0, tiled=True)
    shared = lax.psum_scatter(shared.reshape(-1, rank), "dp", scatter_dimension=0, tiled=True)
    biases = shared[n_head * count :].reshape(-1)
    shared = lax.psum_scatter(
        shared[: n_head * count], "head", scatter_dimension=0, tiled=True
    )
    small = shared[6 * own_rows :].reshape(-1)[: 6 * own_rows].reshape(3, 2, own_rows)
    return (
        layer_output,
        grad_input,
        small[0],
        small[1],
        biases[:n_proj].reshape(3, heads_local, span),
        shared[: 3 * own_rows].reshape(3, own_rows, rank),
        per_head[:, :c1].reshape(factor_rows, 3, head_width).transpose(1, 0, 2),
        per_head[:, c2:c3].T,
        shared[4 * own_rows : 5 * own_rows].T,
        biases[n_proj : n_proj + n_hid].reshape(-1, span),
        shared[3 * own_rows : 4 * own_rows],
        per_head[:, c1:c2],
        per_head[:, c3:].T,
        shared[5 * own_rows : 6 * own_rows].T,
        small[2],
    )


def solution(mesh):
    in_specs = (
        P(("dp", "head"), None),
        P(("dp", "head"), None),
        P("dp"),
        P(None, ("dp", "head")),
        P(None, ("dp", "head")),
        P("dp", None, "head"),
        P(None, "head", "dp"),
        P(None, ("dp", "head"), None),
        P(None, "dp", "head"),
        P("head", "dp"),
        P("head", "dp"),
        P(None, ("dp", "head")),
        P("dp", "head"),
        P("head", "dp"),
        P(("dp", "head"), None),
        P("dp", "head"),
        P("head", "dp"),
        P("head", "dp"),
        P(None, ("dp", "head")),
        P(None, ("dp", "head")),
    )
    out_specs = (
        P(("dp", "head"), None),
        P(("dp", "head"), None),
        P(None, ("dp", "head")),
        P(None, ("dp", "head")),
        P(None, "head", "dp"),
        P(None, ("dp", "head"), None),
        P(None, "dp", "head"),
        P("head", "dp"),
        P(None, ("dp", "head")),
        P("head", "dp"),
        P(("dp", "head"), None),
        P("dp", "head"),
        P("head", "dp"),
        P(None, ("dp", "head")),
        P(None, ("dp", "head")),
    )
    return jax.shard_map(shards, mesh=mesh, in_specs=in_specs, out_specs=out_specs, check_vma=False)
```

time: 2030 us -> 866 us (0.43)
  waiting for transfers between devices: 1090 us -> 433 us
  blocking collectives: 586 us -> 15.5 us
  matrix products: 192 us -> 237 us
    all_gather x14 -> x1, blocking collectives: 562 us -> 15.5 us  [shards(): shared = lax.all_gather(shared, 'head', axis=0, tiled=True)]
    reduce_scatter x9 -> x3, waiting for transfers between devices: 574 us -> 135 us  [the longest x1 77.3 us: shards(): lax.psum_scatter(branch.astype(low), 'head', scatter_dimension=0, tiled=T...]
    unnamed x25 -> x11, waiting for transfers between devices: 520 us -> 92 us
    all_gather x6 -> x4, waiting for transfers between devices: 0.07 us -> 207 us  [the longest x1 76.8 us: shards(): rows_all = lax.all_gather(layer_input_rows, 'head', axis=0, tiled=True)]
    dot_general x32 -> x48, matrix products: 152 us -> 178 us  [the longest x18 76.9 us: mm_t(): lax.dot_general(left, right, (((1,), (1,)), ((), ())), preferred_element_...]
    unnamed x1 -> x0, blocking collectives: 24.2 us -> none
  transfers between devices with their start and end apart: 20 -> 9, of which waited for: 12 -> 9; matrix products, arithmetic and copies ran while one was open for 15% -> 13% of each run, Pallas kernels for 0% -> 0%
where the time goes in v1:
time: 866 us; the launch traced here: 861 us
  waiting for transfers between devices  433 us (50%)
  matrix products  237 us (27%)
  local copies, waits for them, and re-layouts  103 us (12%)
  other arithmetic  52.3 us (6%)
  between operations  16.8 us (2%)
  blocking collectives  15.5 us (2%)
    unnamed x11, waiting for transfers between devices  92 us
    reduce_scatter x1, waiting for transfers between devices, shards(): lax.psum_scatter(branch.astype(low), 'head', scatter_dimension=0, tiled=T...  77.3 us
    dot_general x18, matrix products, mm_t(): lax.dot_general(left, right, (((1,), (1,)), ((), ())), preferred_element_...  76.9 us
    all_gather x1, waiting for transfers between devices, shards(): rows_all = lax.all_gather(layer_input_rows, 'head', axis=0, tiled=True)  76.8 us
    all_gather x1, waiting for transfers between devices, shards(): cot = lax.all_gather(cotangent, 'head', axis=0, tiled=True)  75.7 us
    dot_general x18, matrix products, mm(): return jnp.dot(left, right, preferred_element_type=f32)  74.1 us
    reduce_scatter x1, waiting for transfers between devices, shards(): per_head = lax.psum_scatter(per_head, 'dp', scatter_dimension=0, tiled=True)  39.9 us
    all_gather x1, waiting for transfers between devices, shards(): main = lax.all_gather(main, 'dp', axis=0, tiled=False)  31.5 us
  transfers between devices with their start and end apart: 9, of which 9 were waited for; matrix products, arithmetic and copies ran while one was open for 13% of the time, Pallas kernels for 0%

profile of v1, /device:TPU:0, one launch (start us, length us, event | category | flops | bytes accessed | tf_op | source)
XLA Modules:
  0.0 860.7 jit_solution(12367039019800721248)
XLA Ops:
  11.9 15.5 %all_gather.22 = bf16[832,128]{1,0:T(8,128)(2,1)S(1)} all-gather(bf16[208,128]{1,0:T(8,128)(2,1)S(1)} %constant_dynamic-update-slice_fusion), channel_id=1, replica_groups=mesh['dp'=8,'head'=4] {'head'}, dimensions={0}, use_global_device_ids=true | all-gather | bytes 266240 | tf_op jit(solution)/shard_map/all_gather | solution.py:228
  35.1 22.5 %all-gather.11.cloned.1.call-done = bf16[6784,128]{1,0:T(8,128)(2,1)} async-done(((bf16[848,128]{1,0:T(8,128)(2,1)}), bf16[6784,128]{1,0:T(8,128)(2,1)}) %all-gather.11.cloned.1.call-update) | async-done | bytes 1736720 | tf_op jit(solution)/shard_map/all_gather | solution.py:230
  63.1 76.8 %all-gather.7.cloned.1.call-done = bf16[2048,1024]{1,0:T(8,128)(2,1)} async-done(((bf16[512,1024]{1,0:T(8,128)(2,1)}), bf16[2048,1024]{1,0:T(8,128)(2,1)}) %all-gather.7.cloned.1.call-update) | async-done | bytes 4194320 | tf_op jit(solution)/shard_map/all_gather | solution.py:185
  145.1 75.7 %all-gather.9.cloned.1.call-done = bf16[2048,1024]{1,0:T(8,128)(2,1)} async-done(((bf16[512,1024]{1,0:T(8,128)(2,1)}), bf16[2048,1024]{1,0:T(8,128)(2,1)}) %all-gather.9.cloned.1.call-update) | async-done | bytes 4194320 | tf_op jit(solution)/shard_map/all_gather | solution.py:291
  220.8 4.7 fusion.114
  238.2 31.5 %all-gather.13.cloned.1.call-done = bf16[1152,3072]{1,0:T(8,128)(2,1)} async-done(((bf16[144,3072]{1,0:T(8,128)(2,1)}), bf16[1152,3072]{1,0:T(8,128)(2,1)}) %all-gather.13.cloned.1.call-update) | async-done | bytes 7077904 | tf_op jit(solution)/shard_map/all_gather | solution.py:231
  313.8 29.5 %while.28 = (s32[]{:T(128)}, bf16[2,1024,4,64]{1,3,2,0:T(8,128)(2,1)}, f32[2,2,4,512]{3,2,1,0:T(4,128)S(1)}, bf16[2,1024,4,64]{1,3,2,0:T(8,128)(2,1)}, bf16[2,10...) while((s32[]{:T(128)}, ...), condition=%wide.region_7.8_spmd, body=%wide.region_2.7_spmd.sunk | while | flops 845417472 | bytes 82492136 | solution.py:277
  354.4 65.0 %while.29 = (s32[]{:T(128)}, f32[2,1024,4,64]{1,3,2,0:T(8,128)}, f32[2,1024,4,64]{1,3,2,0:T(8,128)}, bf16[2,1024,4,64]{1,3,2,0:T(8,128)(2,1)}, bf16[2,1024,4,64]...) while((s32[]{:T(128)}, f32[2,1024,4,64]{1,3,2,0:T(8,128)}, ...), condition=%wide.region_14.15_spmd, body=%wide.region_11.14_spmd.sunk | while | flops 2048261120 | bytes 206406688 | solution.py:308
  371.1 4.6 multiply_reduce_fusion.4
  429.3 6.8 fusion.130
  439.4 4.7 fusion.143
  446.4 4.6 fusion.140
  453.7 21.9 %multiply_convert_fusion.2 = (bf16[2048,1024]{1,0:T(8,128)(2,1)}, f32[2048,1024]{1,0:T(8,128)}, f32[2048,1024]{1,0:T(8,128)}) fusion(bf16[2048,128]{1,0:T(8,128)(2,1)S(1)} %copy-done.72, bf16[128,3072]{1,0:T(8,128)(2,1)S(1)} %bitcast.475, f32[2048,1024]{1,0:T(8,128)S(1)} %bitcast.523, f32[1024]{0:T(1024)S(1)} %copy-done.96), kind=kOutput, calls=%fused_computation.137 | convolution fusion | flops 679477248 | bytes 30150656 | tf_op jit(solution)/shard_map/dot_general | solution.py:257
  475.6 12.9 %convert_reduce_fusion.1 = (f32[1024]{0:T(1024)S(1)}, bf16[2048,1024]{1,0:T(8,128)(2,1)}) fusion(f32[2048,1024]{1,0:T(8,128)} %get-tuple-element.345, f32[2048,1024]{1,0:T(8,128)} %get-tuple-element.406, f32[2048,1024]{1,0:T(8,128)S(1)} %fusion.148, bf16[2048,1024]{1,0:T(8,128)(2,1)S(1)} %copy-done.13, bf16[1024,3072]{1,0:T(8,128)(2,1)} %bitcast.447), kind=kOutput, calls=%fused_computation.132 | convolution fusion | flops 4330617856 | bytes 35655680 | tf_op jit(solution)/shard_map/dot_general | solution.py:257
  492.1 6.4 fusion.128
  510.6 4.7 convolution_add_fusion
  515.4 15.3 %fusion.95 = (f32[1024]{0:T(1024)S(1)}, f32[1024]{0:T(1024)S(1)}, f32[1024]{0:T(1024)S(1)}, f32[1024]{0:T(1024)S(1)}, bf16[2048,1024]{1,0:T(8,128)(2,1)}) fusion(bf16[2048,1024]{1,0:T(8,128)(2,1)S(1)} %copy-done.11, f32[2048]{0:T(1024)S(1)} %copy-done.83, f32[2048]{0:T(1024)S(1)} %copy-done.79, f32[2048,1024]{1,0:T(8,128)} %convolution_add_fusion, ...), kind=kOutput, calls=%fused_computation.127 | convolution fusion | flops 1111486464 | bytes 60334080 | tf_op jit(solution)/shard_map/dot_general | solution.py:260
  543.1 8.4 fusion.126
  551.5 9.4 %add_convert_fusion.2 = bf16[2048,1024]{1,0:T(8,128)(2,1)} fusion(f32[2048,1024]{1,0:T(8,128)S(1)} %fusion.175, f32[2048,1024]{1,0:T(8,128)} %fusion.176, f32[2048,1024]{1,0:T(8,128)} %fusion.126, bf16[2048,256]{0,1:T(8,128)(2,1)S(1)} %bitcast.440, bf16[1024,3072]{1,0:T(8,128)(2,1)} %bitcast.451), kind=kOutput, calls=%fused_computation.136 | convolution fusion | flops 1084227584 | bytes 30932992 | tf_op jit(solution)/shard_map/dot_general | solution.py:260
  590.0 17.7 %reduce-scatter.6.cloned.1.call-done = bf16[512,1024]{1,0:T(8,128)(2,1)} async-done(((bf16[2048,1024]{1,0:T(8,128)(2,1)}), bf16[512,1024]{1,0:T(8,128)(2,1)}) %reduce-scatter.6.cloned.1.call-update) | async-done | bytes 1048592 | tf_op jit(solution)/shard_map/reduce_scatter | solution.py:328
  609.8 77.3 %reduce-scatter.4.cloned.1.call-done = bf16[512,1024]{1,0:T(8,128)(2,1)} async-done(((bf16[2048,1024]{1,0:T(8,128)(2,1)}), bf16[512,1024]{1,0:T(8,128)(2,1)}) %reduce-scatter.4.cloned.1.call-update) | async-done | bytes 1048592 | tf_op jit(solution)/shard_map/reduce_scatter | solution.py:286
  711.2 57.5 %all-reduce.11.cloned.1.call-done = f32[6464,128]{1,0:T(8,128)} async-done(((f32[6464,128]{1,0:T(8,128)}), f32[6464,128]{1,0:T(8,128)}) %all-reduce.11.cloned.1.call-update) | async-done | bytes 3309584
  770.5 39.9 %reduce-scatter.8.cloned.1.call-done = f32[16,3072]{1,0:T(8,128)} async-done(((f32[128,3072]{1,0:T(8,128)}), f32[16,3072]{1,0:T(8,128)}) %reduce-scatter.8.cloned.1.call-update) | async-done | bytes 196624 | tf_op jit(solution)/shard_map/reduce_scatter | solution.py:361
  816.8 33.0 %all-reduce.13.cloned.1.call-done = f32[800,128]{1,0:T(8,128)} async-done(((f32[800,128]{1,0:T(8,128)}), f32[800,128]{1,0:T(8,128)}) %all-reduce.13.cloned.1.call-update) | async-done | bytes 409616
  (510 shorter events, 290.5 us)
Async XLA Ops:
  7.3 50.4 %all-gather.11.cloned.1.call-start = ((), (), s32[]{:S(2)}) async-start(), calls=%async_computation.8 | async-start | bytes 1953792 | tf_op jit(solution)/shard_map/all_gather | solution.py:230
  29.8 110.1 %all-gather.7.cloned.1.call-start = ((), (), s32[]{:S(2)}) async-start(), calls=%async_computation.3 | async-start | bytes 5242880 | tf_op jit(solution)/shard_map/all_gather | solution.py:185
  30.6 190.2 %all-gather.9.cloned.1.call-start = ((), (), s32[]{:S(2)}) async-start(), calls=%async_computation.5 | async-start | bytes 5242880 | tf_op jit(solution)/shard_map/all_gather | solution.py:291
  31.3 238.5 %all-gather.13.cloned.1.call-start = ((), (), s32[]{:S(2)}) async-start(), calls=%async_computation.9 | async-start | bytes 7962624 | tf_op jit(solution)/shard_map/all_gather | solution.py:231
  34.2 573.5 %reduce-scatter.6.cloned.1.call-start = ((), (), s32[]{:S(2)}) async-start(), calls=%async_computation.6 | async-start | bytes 5242880 | tf_op jit(solution)/shard_map/reduce_scatter | solution.py:328
  35.1 260.5 %copy-start.76 = (f32[1024,8]{0,1:T(8,128)}, f32[1024,8]{0,1:T(8,128)S(1)}, u32[]{:S(2)}) copy-start(f32[1024,8]{0,1:T(8,128)S(1)} %get-tuple-element.405) | copy-start | bytes 98308
  62.3 165.5 %copy-start.87 = (f32[1,1,1024]{2,1,0:T(1,128)}, f32[1,1,1024]{2,1,0:T(1,128)S(1)}, u32[]{:S(2)}) copy-start(f32[1,1,1024]{2,1,0:T(1,128)S(1)} %get-tuple-element.397) | copy-start | bytes 12292
  62.3 165.5 %copy-start.89 = (f32[1,1,1024]{2,1,0:T(1,128)}, f32[1,1,1024]{2,1,0:T(1,128)S(1)}, u32[]{:S(2)}) copy-start(f32[1,1,1024]{2,1,0:T(1,128)S(1)} %get-tuple-element.399) | copy-start | bytes 12292
  63.0 157.8 %copy-start.55 = (bf16[32,32,128]{2,1,0:T(8,128)(2,1)}, bf16[32,32,128]{2,1,0:T(8,128)(2,1)S(1)}, u32[]{:S(2)}) copy-start(bf16[32,32,128]{2,1,0:T(8,128)(2,1)S(1)} %get-tuple-element.374) | copy-start | bytes 786436
  63.0 162.4 %copy-start.53 = (bf16[32,32,128]{2,1,0:T(8,128)(2,1)}, bf16[32,32,128]{2,1,0:T(8,128)(2,1)S(1)}, u32[]{:S(2)}) copy-start(bf16[32,32,128]{2,1,0:T(8,128)(2,1)S(1)} %get-tuple-element.373) | copy-start | bytes 786436
  63.1 167.1 %copy-start.70 = (bf16[1,32,32,128]{3,2,0,1:T(8,128)(2,1)}, bf16[1,32,32,128]{3,2,0,1:T(8,128)(2,1)S(1)}, u32[]{:S(2)}) copy-start(bf16[1,32,32,128]{3,2,0,1:T(8,128)(2,1)S(1)} %get-tuple-element.380) | copy-start | bytes 786436
  63.1 169.7 %copy-start.68 = (bf16[1,32,32,128]{3,2,0,1:T(8,128)(2,1)}, bf16[1,32,32,128]{3,2,0,1:T(8,128)(2,1)S(1)}, u32[]{:S(2)}) copy-start(bf16[1,32,32,128]{3,2,0,1:T(8,128)(2,1)S(1)} %get-tuple-element.379) | copy-start | bytes 786436
  63.1 171.8 %copy-start.66 = (bf16[1,32,32,128]{3,2,0,1:T(8,128)(2,1)}, bf16[1,32,32,128]{3,2,0,1:T(8,128)(2,1)S(1)}, u32[]{:S(2)}) copy-start(bf16[1,32,32,128]{3,2,0,1:T(8,128)(2,1)S(1)} %get-tuple-element.381) | copy-start | bytes 786436
  143.4 84.4 %copy-start.78 = (f32[2048]{0:T(1024)}, f32[2048]{0:T(1024)S(1)}, u32[]{:S(2)}) copy-start(f32[2048]{0:T(1024)S(1)} %broadcast_multiply_fusion) | copy-start | bytes 24580
  145.0 82.7 %copy-start.82 = (f32[2048]{0:T(1024)}, f32[2048]{0:T(1024)S(1)}, u32[]{:S(2)}) copy-start(f32[2048]{0:T(1024)S(1)} %add_rsqrt_fusion) | copy-start | bytes 24580
  236.2 66.8 %copy-start.59 = (bf16[2048,128]{1,0:T(8,128)(2,1)}, bf16[2048,128]{1,0:T(8,128)(2,1)S(1)}, u32[]{:S(2)}) copy-start(bf16[2048,128]{1,0:T(8,128)(2,1)S(1)} %convolution_convert_fusion.5) | copy-start | bytes 1572868
  439.4 61.8 %copy-start.31 = (bf16[2048,128]{1,0:T(8,128)(2,1)}, bf16[2048,128]{1,0:T(8,128)(2,1)S(1)}, u32[]{:S(2)}) copy-start(bf16[2048,128]{1,0:T(8,128)(2,1)S(1)} %fusion.111) | copy-start | bytes 1572868
  530.7 156.4 %reduce-scatter.4.cloned.1.call-start = ((), (), s32[]{:S(2)}) async-start(), calls=%async_computation.4 | async-start | bytes 5242880 | tf_op jit(solution)/shard_map/reduce_scatter | solution.py:286
  560.9 207.8 %all-reduce.11.cloned.1.call-start = ((), (), s32[]{:S(2)}) async-start(), calls=%async_computation.10 | async-start | bytes 6619136
  586.1 101.0 %copy-start.46 = (bf16[512,1024]{1,0:T(8,128)(2,1)S(1)}, bf16[512,1024]{1,0:T(8,128)(2,1)}, u32[]{:S(2)}) copy-start(bf16[512,1024]{1,0:T(8,128)(2,1)} %param.25) | copy-start | bytes 3145732
  586.1 101.0 %copy-start.91 = (f32[1,1,1024]{2,1,0:T(1,128)S(1)}, f32[1,1,1024]{2,1,0:T(1,128)}, u32[]{:S(2)}) copy-start(f32[1,1,1024]{2,1,0:T(1,128)} %get-tuple-element.394) | copy-start | bytes 12292
  586.1 101.0 %copy-start.92 = (f32[1,1,1024]{2,1,0:T(1,128)S(1)}, f32[1,1,1024]{2,1,0:T(1,128)}, u32[]{:S(2)}) copy-start(f32[1,1,1024]{2,1,0:T(1,128)} %get-tuple-element.395) | copy-start | bytes 12292
  696.5 113.9 %reduce-scatter.8.cloned.1.call-start = ((), (), s32[]{:S(2)}) async-start(), calls=%async_computation.7 | async-start | bytes 1769472 | tf_op jit(solution)/shard_map/reduce_scatter | solution.py:361
  708.6 141.2 %all-reduce.13.cloned.1.call-start = ((), (), s32[]{:S(2)}) async-start(), calls=%async_computation.11 | async-start | bytes 819200
  (101 other events, 606.6 us)
Sparse Core Ops, SparseCore 0:
  29.9 27.6 all-gather.10
  59.2 80.7 all-gather.6
  141.5 79.2 all-gather.8
  222.5 47.1 all-gather.12
  530.8 76.7 reduce-scatter.5
  609.8 77.2 reduce-scatter.3
  696.6 72.0 all-reduce.10
  772.0 38.3 reduce-scatter.7
  812.7 37.0 all-reduce.12
